TPU v7x, 128 devices: a whole 4x4x4 slice. The times are simulated.
128 devices in a mesh: orb: 32 (over y, z, core), row: 4 (over x).
Axes of the slice: x: 4, y: 4, z: 4, core: 2. Of those that a mesh axis runs over, the one named last changes fastest.
Arguments:
- half_ints: bfloat16 [256, 2048, 1536], P(('orb', 'row')), may hold values from -0.125 to 0.125
- metric_inv: bfloat16 [128, 128, 128], P(('orb', 'row')), may hold values from -0.1 to 1.4, as said below
- coefficients: bfloat16 [4096, 256], P(('orb', 'row')), may hold values from -0.15625 to 0.15625
- basis_domain: int32 [256, 12], P(('orb', 'row')), may hold values from 0 to 31, as said below
- aux_domain: int32 [256, 16], P(('orb', 'row')), may hold values from 0 to 127, as said below
- aux_count: int32 [256], P(('orb', 'row')), may hold values from 8 to 16, as said below
Outputs:
- exchange_matrix: float32 [4096, 4096], P(('orb', 'row'))
- self_energy: float32 [], replicated
Inputs may be any that keep to these rules, and one draw needn't show every extreme that they name: `metric_inv`: each block is lower triangular. `basis_domain`: each row names 12 different basis blocks. Among the 2 rows of one device (rows d * 2 to (d + 1) * 2 - 1), no basis block is named by more than 1 row (the two orbitals' domains are disjoint). `aux_domain`: each row names 16 different auxiliary blocks. Orbital i uses the first aux_count[i] blocks of its list; some orbital uses all 16.
All inputs are finite; a program needn't handle non-finite values.
Results may differ from a plain program's by a relative error of at most 0.00079.
Values may be sent and summed in bfloat16 or wider, within the bound.
A program may use at most 128 MiB of HBM per device.

v0:
```python
import jax
import jax.numpy as jnp
from jax import lax
from jax.sharding import PartitionSpec as P


def orbital_terms(block_rows, aux_ids, live_count, basis_ids, coef_column, metric_all):
    block_width = metric_all.shape[1]
    columns = block_rows.shape[1]
    group_size = min(4, aux_ids.shape[0])
    basis_blocks = coef_column.shape[0] // block_width
    coef_domain = coef_column.reshape(basis_blocks, block_width)[basis_ids].reshape(-1)
    group_total = (live_count + group_size - 1) // group_size

    def advance(group_index, carry):
        k_partial, energy = carry
        first_block = group_index * group_size
        rows_now = lax.dynamic_slice_in_dim(
            block_rows, first_block * block_width, group_size * block_width, 0
        )
        rows_now = rows_now.reshape(group_size, block_width, columns)
        factors = metric_all[lax.dynamic_slice_in_dim(aux_ids, first_block, group_size, 0)]
        fitted = jnp.einsum(
            "gqp,gpm->gqm", factors, rows_now, preferred_element_type=jnp.float32
        ).astype(jnp.bfloat16)
        live_mask = first_block + jnp.arange(group_size, dtype=jnp.int32) < live_count
        fitted = jnp.where(live_mask[:, None, None], fitted, jnp.zeros_like(fitted))
        flat_rows = fitted.reshape(group_size * block_width, columns)
        k_partial = k_partial + lax.dot_general(
            flat_rows, flat_rows, (((0,), (0,)), ((), ())), preferred_element_type=jnp.float32
        )
        projected = jnp.dot(flat_rows, coef_domain, preferred_element_type=jnp.float32)
        return (k_partial, energy + jnp.sum(projected * projected))

    initial = (jnp.zeros((columns, columns), jnp.float32), jnp.zeros((), jnp.float32))
    return lax.fori_loop(0, group_total, advance, initial)


def per_device(half_ints, metric_inv, coefficients, basis_domain, aux_domain, aux_count):
    devices = lax.axis_size(("orb", "row"))
    orb_local = half_ints.shape[0]
    block_width = metric_inv.shape[1]
    rows_local = coefficients.shape[0]
    basis_total = rows_local * devices
    basis_blocks = basis_total // block_width
    count_blocks = basis_domain.shape[1]
    metric_all = lax.all_gather(metric_inv, ("orb", "row"), axis=0, tiled=True)
    split_rows = coefficients.reshape(rows_local, devices, orb_local)
    coef_own = lax.all_to_all(
        split_rows, ("orb", "row"), split_axis=1, concat_axis=0, tiled=True
    ).reshape(basis_total, orb_local)
    members = [
        (
            half_ints[orbital],
            aux_domain[orbital],
            aux_count[orbital],
            basis_domain[orbital],
            coef_own[:, orbital],
        )
        for orbital in range(orb_local)
    ]
    k_list = []
    domain_list = []
    energy_sum = jnp.zeros((), jnp.float32)
    for member in members:
        k_partial, energy = orbital_terms(
            member[0], member[1], member[2], member[3], member[4], metric_all
        )
        k_list.append(k_partial.astype(jnp.bfloat16))
        domain_list.append(member[3])
        energy_sum = energy_sum + energy
    energy_high = energy_sum.astype(jnp.bfloat16)
    energy_low = (energy_sum - energy_high.astype(jnp.float32)).astype(jnp.bfloat16)
    energy_pair = jnp.stack([energy_high, energy_low], 0)
    energy_out = jnp.broadcast_to(energy_pair[None, :], (devices, 2))
    columns = k_list[0].shape[1]
    domains = jnp.stack(domain_list, 0)
    block_range = jnp.arange(basis_blocks, dtype=jnp.int32)
    slots = -(-(orb_local * count_blocks) // basis_blocks) + 0
    slots = min(slots, orb_local)
    span = block_width // rows_local
    hits = (domains[:, :, None] == block_range[None, None, :]).astype(jnp.int32)
    cover = jnp.sum(hits, 1)
    earlier = jnp.cumsum(cover, 0) - cover
    slot_hot = (earlier[:, :, None] == jnp.arange(slots, dtype=jnp.int32)[None, None, :]).astype(
        jnp.int32
    )
    select = hits.transpose(2, 0, 1)[:, None, :, :] * slot_hot.transpose(1, 2, 0)[:, :, :, None]
    occupied = jnp.sum(select, 3)
    slot_ids = jnp.sum(occupied[:, :, :, None] * domains[None, None, :, :], 2)
    k_stack = jnp.stack(k_list, 0).reshape(orb_local, count_blocks, span, rows_local, columns)
    compact = jnp.einsum(
        "bsok,oktrc->btsrc",
        select.astype(jnp.bfloat16),
        k_stack,
        preferred_element_type=jnp.bfloat16,
    ).reshape(devices, slots, rows_local, columns)
    compact_ids = jnp.broadcast_to(slot_ids[:, None], (basis_blocks, span, slots, count_blocks))
    compact_ids = compact_ids.reshape(devices, slots, count_blocks).astype(jnp.bfloat16)
    arrived, arrived_ids, energy_in = (
        lax.all_to_all(compact, ("orb", "row"), split_axis=0, concat_axis=0, tiled=True),
        lax.all_to_all(compact_ids, ("orb", "row"), split_axis=0, concat_axis=0, tiled=True),
        lax.all_to_all(energy_out, ("orb", "row"), split_axis=0, concat_axis=0, tiled=True),
    )
    slot_count = arrived.shape[1]
    arrived = arrived.reshape(devices, slot_count, rows_local, count_blocks, block_width)
    place_columns = (
        arrived_ids.astype(jnp.float32)[..., None] == jnp.arange(basis_blocks, dtype=jnp.float32)
    ).astype(jnp.bfloat16)
    k_rows = jnp.einsum(
        "sorkc,sokb->rbc", arrived, place_columns, preferred_element_type=jnp.float32
    ).reshape(rows_local, basis_total)
    energy_total = jnp.sum(energy_in.astype(jnp.float32))
    return (k_rows, energy_total / (orb_local * devices))


def solution(mesh):
    in_specs = (
        P(("orb", "row"), None, None),
        P(("orb", "row"), None, None),
        P(("orb", "row"), None),
        P(("orb", "row"), None),
        P(("orb", "row"), None),
        P(("orb", "row")),
    )
    out_specs = (P(("orb", "row"), None), P())
    return jax.shard_map(
        per_device, mesh=mesh, in_specs=in_specs, out_specs=out_specs, check_vma=False
    )
```

profile of v0, /device:TPU:1, one launch (start us, length us, event | category | flops | bytes accessed | tf_op | source)
XLA Modules:
  0.0 464.2 jit_solution(11396541130770513502)
XLA Ops:
  7.9 1.5 copy.74
  9.3 11.5 %all-to-all-start.1 = ((bf16[32,128,2]{0,2,1:T(2,128)(2,1)}), bf16[32,128,2]{0,2,1:T(2,128)(2,1)S(1)}, u32[]{:S(2)}, u32[]{:S(2)}) async-start(bf16[32,128,2]{0,2,1:T(2,128)(2,1)} %bitcast.17), calls=%async_computation.1 | async-start | bytes 131072 | tf_op jit(solution)/shard_map/all_to_all | solution.py:49
  23.5 10.3 %slice_bitcast_fusion.1 = (bf16[2048,1536]{1,0:T(8,128)(2,1)}, bf16[2048,1536]{1,0:T(8,128)(2,1)}) fusion(bf16[2,2048,1536]{2,1,0:T(8,128)(2,1)} %param.10), kind=kLoop, calls=%fused_computation.26 | loop fusion | bytes 25165824 | tf_op jit(solution)/shard_map/squeeze | solution.py:54
  36.5 9.8 %all-to-all-start = ((bf16[128,1,12]{2,1,0:T(2,128)(2,1)}), bf16[128,1,12]{2,1,0:T(2,128)(2,1)S(1)}, u32[]{:S(2)}, u32[]{:S(2)}) async-start(bf16[128,1,12]{2,1,0:T(2,128)(2,1)} %copy.72), calls=%async_computation | async-start | bytes 131072 | tf_op jit(solution)/shard_map/all_to_all | solution.py:102
  47.6 33.6 %all-gather.2.cloned.1.call-done = bf16[128,128,128]{2,1,0:T(8,128)(2,1)} async-done(((bf16[1,128,128]{2,1,0:T(8,128)(2,1)}), bf16[128,128,128]{2,1,0:T(8,128)(2,1)}) %all-gather.2.cloned.1.call-update) | async-done | bytes 4194320 | tf_op jit(solution)/shard_map/all_gather | solution.py:47
  81.3 4.8 %broadcast.186.clone = f32[1536,1536]{1,0:T(8,128)} broadcast(f32[]{:T(128)} %copy.110), dimensions={} | broadcast | bytes 9437188 | tf_op jit(solution)/shard_map/broadcast.15
  86.1 30.1 %while.29 = (s32[]{:T(128)}, f32[1536,1536]{1,0:T(8,128)}, f32[]{:T(128)}, s32[]{:T(128)}, s32[]{:T(128)}, /*index=5*/s32[16]{0:T(128)S(1)}, bf16[128,128,128]{2...) while((s32[]{:T(128)}, f32[1536,1536]{1,0:T(8,128)}, ...), condition=%wide.region_9.10_spmd, body=%wide.region_7.9_spmd.sunk | while | flops 2622752768 | bytes 28722520 | solution.py:36
  86.2 2.8 gather_fusion.1
  89.0 1.5 constant_dynamic-slice_fusion.5
  91.7 7.7 %bitcast_add_fusion.5 = f32[1536,1536]{1,0:T(8,128)} fusion(f32[1536,1536]{1,0:T(8,128)} %get-tuple-element.416, bf16[4,128,1536]{2,1,0:T(8,128)(2,1)S(1)} %fusion.71), kind=kOutput, calls=%fused_computation.12.clone.1 | convolution fusion | flops 2418278400 | bytes 20447232 | tf_op jit(solution)/shard_map/while/body/dot_general | solution.py:29
  101.3 2.8 gather_fusion.1
  104.1 1.5 constant_dynamic-slice_fusion.5
  106.8 7.7 %bitcast_add_fusion.5 = f32[1536,1536]{1,0:T(8,128)} fusion(f32[1536,1536]{1,0:T(8,128)} %get-tuple-element.416, bf16[4,128,1536]{2,1,0:T(8,128)(2,1)S(1)} %fusion.71), kind=kOutput, calls=%fused_computation.12.clone.1 | convolution fusion | flops 2418278400 | bytes 20447232 | tf_op jit(solution)/shard_map/while/body/dot_general | solution.py:29
  116.3 4.8 %broadcast.186.clone.1 = f32[1536,1536]{1,0:T(8,128)} broadcast(f32[]{:T(128)} %copy.110), dimensions={} | broadcast | bytes 9437188 | tf_op jit(solution)/shard_map/broadcast.15
  121.1 29.9 %while.28 = (s32[]{:T(128)}, f32[1536,1536]{1,0:T(8,128)}, f32[]{:T(128)}, s32[]{:T(128)}, s32[]{:T(128)}, /*index=5*/s32[16]{0:T(128)S(1)}, bf16[128,128,128]{2...) while((s32[]{:T(128)}, f32[1536,1536]{1,0:T(8,128)}, ...), condition=%wide.region_6.7_spmd, body=%wide.region_4.6_spmd.sunk | while | flops 2622752768 | bytes 28722520 | solution.py:36
  121.2 2.8 gather_fusion
  123.9 1.5 constant_dynamic-slice_fusion.4
  126.7 7.5 %bitcast_add_fusion.4 = f32[1536,1536]{1,0:T(8,128)} fusion(f32[1536,1536]{1,0:T(8,128)} %get-tuple-element.461, bf16[4,128,1536]{2,1,0:T(8,128)(2,1)S(1)} %fusion.63), kind=kOutput, calls=%fused_computation.4.clone.1 | convolution fusion | flops 2418278400 | bytes 20447232 | tf_op jit(solution)/shard_map/while/body/dot_general | solution.py:29
  136.0 2.8 gather_fusion
  138.8 1.5 constant_dynamic-slice_fusion.4
  141.5 7.5 %bitcast_add_fusion.4 = f32[1536,1536]{1,0:T(8,128)} fusion(f32[1536,1536]{1,0:T(8,128)} %get-tuple-element.461, bf16[4,128,1536]{2,1,0:T(8,128)(2,1)S(1)} %fusion.63), kind=kOutput, calls=%fused_computation.4.clone.1 | convolution fusion | flops 2418278400 | bytes 20447232 | tf_op jit(solution)/shard_map/while/body/dot_general | solution.py:29
  151.1 4.4 convert_element_type.74
  155.5 5.5 %copy.77 = bf16[1,12,4,32,1536]{4,1,0,3,2:T(8,128)(2,1)} copy(bf16[1,12,4,32,1536]{4,3,2,1,0:T(8,128)(2,1)S(1)} %bitcast.139) | data formatting | bytes 9437184 | tf_op jit(solution)/shard_map/stack | solution.py:91
  161.7 5.5 %copy.76 = bf16[1,12,4,32,1536]{4,1,0,3,2:T(8,128)(2,1)} copy(bf16[1,12,4,32,1536]{4,3,2,1,0:T(8,128)(2,1)S(1)} %bitcast.140) | data formatting | bytes 9437184 | tf_op jit(solution)/shard_map/stack | solution.py:91
  167.8 64.1 %all-to-all-start.3 = ((bf16[128,1,2]{2,1,0:T(2,128)(2,1)}), bf16[128,1,2]{2,1,0:T(2,128)(2,1)S(1)}, u32[]{:S(2)}, u32[]{:S(2)}) async-start(bf16[128,1,2]{2,1,0:T(2,128)(2,1)} %broadcast_in_dim.59), calls=%async_computation.3 | async-start | bytes 131072 | tf_op jit(solution)/shard_map/all_to_all | solution.py:103
  231.9 7.0 %fusion.6 = bf16[32,4,1,32,1536]{4,0,3,1,2:T(8,128)(2,1)S(1)} fusion(bf16[1,12,4,32,1536]{4,1,0,3,2:T(8,128)(2,1)} %copy.77, bf16[1,12,4,32,1536]{4,1,0,3,2:T(8,128)(2,1)} %copy.76, s32[32,2]{0,1:T(2,128)S(1)} %fusion.20, s32[2,12]{1,0:T(2,128)S(1)} %copy-done), kind=kOutput, calls=%fused_computation.24 | convolution fusion | flops 306710784 | bytes 22020448 | tf_op jit(solution)/shard_map/bsok,oktrc->btsrc/dot_general | solution.py:92
  239.0 22.3 %copy.78 = bf16[32,4,1,32,1536]{4,3,1,0,2:T(8,128)(2,1)} copy(bf16[32,4,1,32,1536]{4,0,3,1,2:T(8,128)(2,1)S(1)} %fusion.6) | data formatting | bytes 25165824 | tf_op jit(solution)/shard_map/bsok,oktrc->btsrc/transpose | solution.py:92
  261.3 10.2 %all-to-all-start.2 = ((bf16[128,1,32,1536]{3,2,1,0:T(8,128)(2,1)}), bf16[128,1,32,1536]{3,2,1,0:T(8,128)(2,1)}, u32[]{:S(2)}, u32[]{:S(2)}) async-start(bf16[128,1,32,1536]{3,2,1,0:T(8,128)(2,1)} %bitcast.137), calls=%async_computation.2 | async-start | bytes 25165824 | tf_op jit(solution)/shard_map/all_to_all | solution.py:101
  273.0 158.9 %all-to-all-done.2 = bf16[128,1,32,1536]{3,2,1,0:T(8,128)(2,1)} async-done(((bf16[128,1,32,1536]{3,2,1,0:T(8,128)(2,1)}), bf16[128,1,32,1536]{3,2,1,0:T(8,128)(2,1)}, u32[]{:S(2)}, u32[]{:S(2)}) %all-to-all-start.2) | async-done | bytes 12582944 | tf_op jit(solution)/shard_map/all_to_all | solution.py:101
  431.8 16.7 %copy.80 = bf16[128,1,32,1536]{0,3,2,1:T(8,128)(2,1)} copy(bf16[128,1,32,1536]{3,2,1,0:T(8,128)(2,1)} %all-to-all-done.2) | data formatting | bytes 25165824 | tf_op jit(solution)/shard_map/all_to_all | solution.py:101
  448.6 6.6 %fusion.10 = f32[32,32,128,1]{2,0,3,1:T(8,128)S(1)} fusion(bf16[128,32,12,128]{0,3,2,1:T(8,128)(2,1)} %bitcast.138, f32[128,12]{0,1:T(8,128)S(1)} %copy.73), kind=kOutput, calls=%fused_computation.30 | convolution fusion | flops 402702336 | bytes 13113344 | tf_op jit(solution)/shard_map/sorkc,sokb->rbc/dot_general | solution.py:110
  455.1 1.1 copy.91
  (70 shorter events, 17.9 us)
Async XLA Ops:
  7.2 74.1 %all-gather.2.cloned.1.call-start = ((), (), s32[]{:S(2)}) async-start(), calls=%async_computation.4 | async-start | bytes 4227072 | tf_op jit(solution)/shard_map/all_gather | solution.py:47
  9.3 27.2 %all-to-all-start.1 = ((bf16[32,128,2]{0,2,1:T(2,128)(2,1)}), bf16[32,128,2]{0,2,1:T(2,128)(2,1)S(1)}, u32[]{:S(2)}, u32[]{:S(2)}) async-start(bf16[32,128,2]{0,2,1:T(2,128)(2,1)} %bitcast.17), calls=%async_computation.1 | async-start | bytes 131072 | tf_op jit(solution)/shard_map/all_to_all | solution.py:49
  23.5 10.3 %copy-start.1 = (s32[2]{0:T(128)S(1)}, s32[2]{0:T(128)}, u32[]{:S(2)}) copy-start(s32[2]{0:T(128)} %param.15) | copy-start | bytes 28
  36.5 130.6 %all-to-all-start = ((bf16[128,1,12]{2,1,0:T(2,128)(2,1)}), bf16[128,1,12]{2,1,0:T(2,128)(2,1)S(1)}, u32[]{:S(2)}, u32[]{:S(2)}) async-start(bf16[128,1,12]{2,1,0:T(2,128)(2,1)} %copy.72), calls=%async_computation | async-start | bytes 131072 | tf_op jit(solution)/shard_map/all_to_all | solution.py:102
  151.1 10.0 %slice-start = ((s8[9437184]{0:T(1024)(128)(4,1)}), s8[4194304]{0:T(1024)(128)(4,1)S(1)}, s32[]{:S(2)}) async-start(s8[9437184]{0:T(1024)(128)(4,1)} %bitcast.131), calls=%async_computation.5 | async-start | bytes 8388608
  151.1 10.0 %slice-start.1 = ((s8[9437184]{0:T(1024)(128)(4,1)}), s8[4194304]{0:T(1024)(128)(4,1)S(1)}, s32[]{:S(2)}) async-start(s8[9437184]{0:T(1024)(128)(4,1)} %bitcast.131), calls=%async_computation.6 | async-start | bytes 8388608
  155.5 5.5 %slice-start.2 = ((s8[9437184]{0:T(1024)(128)(4,1)}), s8[1048576]{0:T(1024)(128)(4,1)S(1)}, s32[]{:S(2)}) async-start(s8[9437184]{0:T(1024)(128)(4,1)} %bitcast.131), calls=%async_computation.7 | async-start | bytes 2097152
  161.6 70.3 %copy-start = (s32[2,12]{1,0:T(2,128)S(1)}, s32[2,12]{1,0:T(2,128)}, u32[]{:S(2)}) copy-start(s32[2,12]{1,0:T(2,128)} %param.13) | copy-start | bytes 292
  167.8 93.5 %all-to-all-start.3 = ((bf16[128,1,2]{2,1,0:T(2,128)(2,1)}), bf16[128,1,2]{2,1,0:T(2,128)(2,1)S(1)}, u32[]{:S(2)}, u32[]{:S(2)}) async-start(bf16[128,1,2]{2,1,0:T(2,128)(2,1)} %broadcast_in_dim.59), calls=%async_computation.3 | async-start | bytes 131072 | tf_op jit(solution)/shard_map/all_to_all | solution.py:103
  261.3 170.5 %all-to-all-start.2 = ((bf16[128,1,32,1536]{3,2,1,0:T(8,128)(2,1)}), bf16[128,1,32,1536]{3,2,1,0:T(8,128)(2,1)}, u32[]{:S(2)}, u32[]{:S(2)}) async-start(bf16[128,1,32,1536]{3,2,1,0:T(8,128)(2,1)} %bitcast.137), calls=%async_computation.2 | async-start | bytes 25165824 | tf_op jit(solution)/shard_map/all_to_all | solution.py:101
Sparse Core Ops, SparseCore 0:
  11.1 70.1 all-gather.1
where the time goes:
time: 473 us; the launch traced here: 464 us
  waiting for transfers between devices  193 us (41%)
  starting transfers between devices  95.6 us (20%)
  local copies, waits for them, and re-layouts  94.8 us (20%)
  matrix products  48.2 us (10%)
  between operations  17.3 us (4%)
  other arithmetic  12.2 us (3%)
    all_to_all x1, waiting for transfers between devices, per_device(): lax.all_to_all(compact, ('orb', 'row'), split_axis=0, concat_axis=0, tile...  159 us
    all_to_all x1, starting transfers between devices, per_device(): lax.all_to_all(energy_out, ('orb', 'row'), split_axis=0, concat_axis=0, t...  64.1 us
    all_gather x1, waiting for transfers between devices, per_device(): metric_all = lax.all_gather(metric_inv, ('orb', 'row'), axis=0, tiled=True)  33.6 us
    dot_general x4, matrix products, advance(): lax.dot_general(flat_rows, flat_rows, (((0,), (0,)), ((), ())), preferred...  30.3 us
    transpose x1, local copies, waits for them, and re-layouts, per_device(): jnp.einsum('bsok,oktrc->btsrc', select.astype(jnp.bfloat16), k_stack, pre...  22.3 us
    all_to_all x1, local copies, waits for them, and re-layouts, per_device(): lax.all_to_all(compact, ('orb', 'row'), split_axis=0, concat_axis=0, tile...  16.7 us
    all_to_all x1, starting transfers between devices, per_device(): lax.all_to_all(split_rows, ('orb', 'row'), split_axis=1, concat_axis=0, t...  11.5 us
    gather x4, local copies, waits for them, and re-layouts, advance(): metric_all[lax.dynamic_slice_in_dim(aux_ids, first_block, group_size, 0)]  11 us
  transfers between devices with their start and end apart: 5, of which 2 were waited for; matrix products, arithmetic and copies ran while one was open for 28% of the time, Pallas kernels for 0%

commit v1 on v0

v1 whole, which is shorter than its diff:
```python
import functools

import jax
import jax.numpy as jnp
from jax import lax
from jax.experimental import pallas as pl
from jax.experimental.pallas import tpu as pltpu
from jax.sharding import PartitionSpec as P

AXES = ("orb", "row")


def fit_kernel(shape, dom_ref, aux_ref, count_ref, half_ref, metric_ref, coef_ref, send_ref, energy_ref, fitted, coef_dom):
    orbs, aux_n, dom_n, width, span = shape
    step = pl.program_id(0)
    columns = dom_n * width
    fit_steps = orbs * aux_n

    @pl.when(step == 0)
    def _():
        energy_ref[...] = jnp.zeros_like(energy_ref)
        for orb in range(orbs):
            for k in range(dom_n):
                coef_dom[orb, :, k * width : (k + 1) * width] = coef_ref[orb, dom_ref[orb, k]]

    @pl.when(step < fit_steps)
    def _():
        orb = step // aux_n
        a = step % aux_n
        factor = metric_ref[aux_ref[orb, a]]
        block = jnp.dot(factor, half_ref[0], preferred_element_type=jnp.float32)
        block = jnp.where(a < count_ref[orb], block, 0.0).astype(jnp.bfloat16)
        rows = pl.ds(pl.multiple_of(a * width, width), width)
        fitted[orb, rows, 0:columns] = block
        fitted[orb, rows, columns:] = block[:, 0 : (span - 1) * width]
        weighted = block.astype(jnp.float32) * coef_dom[orb]
        projected = jnp.sum(weighted, axis=1, keepdims=True)
        energy_ref[...] += jnp.sum(projected * projected, axis=0, keepdims=True)

    @pl.when(step >= fit_steps)
    def _():
        orb = (step - fit_steps) // dom_n
        k = (step - fit_steps) % dom_n
        left = fitted[orb, :, pl.ds(pl.multiple_of(k * width, width), width)]
        right = fitted[orb, :, pl.ds(pl.multiple_of(k * width, width), span * width)]
        out = lax.dot_general(left, right, (((0,), (0,)), ((), ())), preferred_element_type=jnp.float32)
        send_ref[0] = out.astype(jnp.bfloat16)


def fit_rows(half_ints, metric_all, coef_blocks, basis_domain, aux_domain, aux_count, basis_blocks):
    orbs, aux_rows, columns = half_ints.shape
    width = metric_all.shape[1]
    aux_n, dom_n = aux_domain.shape[1], basis_domain.shape[1]
    span = dom_n // 2 + 1
    fit_steps = orbs * aux_n
    steps = fit_steps + orbs * dom_n

    def half_map(step, dom, aux, count):
        at = jnp.minimum(step, fit_steps - 1)
        return (at // aux_n, at % aux_n, 0)

    def send_map(step, dom, aux, count):
        at = jnp.maximum(step - fit_steps, 0)
        return (dom[at // dom_n, at % dom_n], 0, 0)

    return pl.pallas_call(
        functools.partial(fit_kernel, (orbs, aux_n, dom_n, width, span)),
        grid_spec=pltpu.PrefetchScalarGridSpec(
            num_scalar_prefetch=3,
            grid=(steps,),
            in_specs=[
                pl.BlockSpec((1, width, columns), half_map),
                pl.BlockSpec(memory_space=pltpu.VMEM),
                pl.BlockSpec(memory_space=pltpu.VMEM),
            ],
            out_specs=[
                pl.BlockSpec((1, width, span * width), send_map),
                pl.BlockSpec((1, 1), lambda step, dom, aux, count: (0, 0)),
            ],
            scratch_shapes=[
                pltpu.VMEM((orbs, aux_rows, columns + (span - 1) * width), jnp.bfloat16),
                pltpu.VMEM((orbs, 1, columns), jnp.float32),
            ],
        ),
        out_shape=[
            jax.ShapeDtypeStruct((basis_blocks, width, span * width), jnp.bfloat16),
            jax.ShapeDtypeStruct((1, 1), jnp.float32),
        ],
        compiler_params=pltpu.CompilerParams(
            vmem_limit_bytes=56 * 1024 * 1024, dimension_semantics=("arbitrary",)
        ),
        name="fit_rows",
    )(basis_domain, aux_domain, aux_count, half_ints, metric_all, coef_blocks)


def gather_rows_kernel(batch, span, half_last, ids_ref, arrived_ref, total_ref, turned_ref, acc):
    step = pl.program_id(0)
    blocks = acc.shape[0] - 1
    rows, width = acc.shape[1], acc.shape[2]
    quarters = width // rows

    @pl.when(step == 0)
    def _():
        acc[...] = jnp.zeros_like(acc)

    for s in range(batch):
        for j in range(span):
            where = ids_ref[step * batch + s, j]
            part = arrived_ref[s, :, j * width : (j + 1) * width].astype(jnp.float32)
            if j == 0 or (half_last and j == span - 1):
                part = part * 0.5
            acc[where] += part

    @pl.when(step == pl.num_programs(0) - 1)
    def _():
        for block in range(blocks):
            total_ref[:, block * width : (block + 1) * width] = acc[block]
        for group in range(blocks // quarters):
            tall = acc[group * quarters : (group + 1) * quarters].reshape(quarters * rows, width)
            turned = tall.T
            for beta in range(quarters):
                piece = turned[:, beta * rows : (beta + 1) * rows]
                for q in range(quarters):
                    tile = piece[q * rows : (q + 1) * rows]
                    packed = jnp.concatenate(
                        [tile[a * 8 : (a + 1) * 8] for a in range(rows // 8)], axis=1
                    )
                    turned_ref[(group * quarters + beta) * quarters + q] = packed


def gather_rows(ids, arrived, basis_blocks, half_last):
    devices, rows, columns = arrived.shape
    span = ids.shape[1]
    width = columns // span
    batch = 8
    return pl.pallas_call(
        functools.partial(gather_rows_kernel, batch, span, half_last),
        grid_spec=pltpu.PrefetchScalarGridSpec(
            num_scalar_prefetch=1,
            grid=(devices // batch,),
            in_specs=[pl.BlockSpec((batch, rows, columns), lambda step, ids: (step, 0, 0))],
            out_specs=[
                pl.BlockSpec((rows, basis_blocks * width), lambda step, ids: (0, 0)),
                pl.BlockSpec((devices, 8, width), lambda step, ids: (0, 0, 0)),
            ],
            scratch_shapes=[pltpu.VMEM((basis_blocks + 1, rows, width), jnp.float32)],
        ),
        out_shape=[
            jax.ShapeDtypeStruct((rows, basis_blocks * width), jnp.float32),
            jax.ShapeDtypeStruct((devices, 8, width), jnp.float32),
        ],
        compiler_params=pltpu.CompilerParams(dimension_semantics=("arbitrary",)),
        name="gather_rows",
    )(ids, arrived)


def finish_kernel(total_ref, tiles_ref, out_ref):
    rows, columns = total_ref.shape
    width = tiles_ref.shape[2]
    quarters = width // rows
    for block in range(columns // width):
        for a in range(rows // 8):
            strip = jnp.concatenate(
                [
                    tiles_ref[block * quarters + q, :, a * rows : (a + 1) * rows]
                    for q in range(quarters)
                ],
                axis=1,
            )
            at = slice(a * 8, (a + 1) * 8), slice(block * width, (block + 1) * width)
            out_ref[at] = total_ref[at] + strip


def finish(total, tiles):
    return pl.pallas_call(
        finish_kernel,
        out_shape=jax.ShapeDtypeStruct(total.shape, jnp.float32),
        name="finish",
    )(total, tiles)


def per_device(half_ints, metric_inv, coefficients, basis_domain, aux_domain, aux_count):
    devices = lax.axis_size(AXES)
    me = lax.axis_index(AXES)
    orbs = half_ints.shape[0]
    width = metric_inv.shape[1]
    rows = coefficients.shape[0]
    basis_blocks = rows * devices // width
    quarters = width // rows
    dom_n = basis_domain.shape[1]
    span = dom_n // 2 + 1

    metric_all = lax.all_gather(metric_inv, AXES, axis=0, tiled=True)
    coef_send = coefficients.T.reshape(devices, orbs * rows)
    dom_send = jnp.broadcast_to(
        basis_domain.reshape(1, orbs * dom_n).astype(jnp.bfloat16), (devices, orbs * dom_n)
    )
    small = jnp.concatenate([coef_send, dom_send], axis=1)
    small = lax.all_to_all(small, AXES, split_axis=0, concat_axis=0, tiled=True)
    coef_own = small[:, : orbs * rows].reshape(devices, orbs, rows).transpose(1, 0, 2)
    coef_blocks = coef_own.reshape(orbs, basis_blocks, 1, width).astype(jnp.float32)
    domains = small[:, orbs * rows :].astype(jnp.int32).reshape(devices, orbs, dom_n)

    send, energy = fit_rows(
        half_ints, metric_all, coef_blocks, basis_domain, aux_domain, aux_count, basis_blocks
    )
    arrived = lax.all_to_all(
        send.reshape(devices, rows, span * width), AXES, split_axis=0, concat_axis=0, tiled=True
    )
    energies = lax.all_to_all(
        jnp.broadcast_to(energy, (devices, 1)), AXES, split_axis=0, concat_axis=0, tiled=True
    )
    mine = me // quarters
    hits = (domains == mine).astype(jnp.int32)
    ids = jnp.stack(
        [jnp.sum(hits * (jnp.roll(domains, -j, axis=2) - basis_blocks), axis=(1, 2)) for j in range(span)],
        axis=1,
    ) + basis_blocks
    total, turned = gather_rows(ids, arrived, basis_blocks, dom_n % 2 == 0)
    tiles = lax.all_to_all(turned, AXES, split_axis=0, concat_axis=0, tiled=True)
    return finish(total, tiles), jnp.sum(energies) / (orbs * devices)


def solution(mesh):
    in_specs = (
        P(AXES, None, None),
        P(AXES, None, None),
        P(AXES, None),
        P(AXES, None),
        P(AXES, None),
        P(AXES),
    )
    out_specs = (P(AXES, None), P())
    return jax.shard_map(
        per_device, mesh=mesh, in_specs=in_specs, out_specs=out_specs, check_vma=False
    )
```

time: 473 us -> 282 us (0.60); the launches traced: 464 us -> 281 us
  local copies, waits for them, and re-layouts: 94.8 us -> 4.34 us
  starting transfers between devices: 95.6 us -> 23 us
  Pallas kernels: 0 us -> 63.6 us
  matrix products: 48.2 us -> 0 us
  waiting for transfers between devices: 193 us -> 151 us
  blocking collectives: 0 us -> 21.2 us
  other arithmetic: 12.2 us -> 2.16 us
    all_to_all x4 -> x3, starting transfers between devices: 95.5 us -> 23 us  [the longest x1 9.65 us: per_device(): lax.all_to_all(turned, AXES, split_axis=0, concat_axis=0, tiled=True)]
    pallas_call x0 -> x3, Pallas kernels: none -> 63.6 us  [the longest x1 46.9 us: fit_rows(): pl.pallas_call(functools.partial(fit_kernel, (orbs, aux_n, dom_n, width,...]
    all_to_all x4 -> x3, waiting for transfers between devices: 159 us -> 100 us  [the longest x1 87.8 us: per_device(): lax.all_to_all(send.reshape(devices, rows, span * width), AXES, split_axi...]
    dot_general x14 -> x0, matrix products: 48.2 us -> none  [the longest x4 30.3 us: advance(): lax.dot_general(flat_rows, flat_rows, (((0,), (0,)), ((), ())), preferred...]
    transpose x1, local copies, waits for them, and re-layouts: 22.3 us -> 0.83 us  [per_device(): coef_send = coefficients.T.reshape(devices, orbs * rows)]
    all_to_all x0 -> x1, blocking collectives: none -> 21.2 us  [per_device(): small = lax.all_to_all(small, AXES, split_axis=0, concat_axis=0, tiled=True)]
    another operation x8 -> x2, local copies, waits for them, and re-layouts: 20.7 us -> 0.14 us  [per_device(): jnp.stack([jnp.sum(hits * (jnp.roll(domains, -j, axis=2) - basis_blocks),...]
    all_to_all x3 -> x2, local copies, waits for them, and re-layouts: 16.8 us -> 0.15 us  [per_device(): small = lax.all_to_all(small, AXES, split_axis=0, concat_axis=0, tiled=True)]
  transfers between devices with their start and end apart: 5 -> 4, of which waited for: 2 -> 3; matrix products, arithmetic and copies ran while one was open for 28% -> 2% of each run, Pallas kernels for 0% -> 5%
where the time goes in v1:
time: 282 us; the launch traced here: 281 us
  waiting for transfers between devices  151 us (54%)
  Pallas kernels  63.6 us (23%)
  starting transfers between devices  23 us (8%)
  blocking collectives  21.2 us (8%)
  between operations  16.1 us (6%)
  local copies, waits for them, and re-layouts  4.34 us (2%)
    all_to_all x1, waiting for transfers between devices, per_device(): lax.all_to_all(send.reshape(devices, rows, span * width), AXES, split_axi...  87.8 us
    all_gather x1, waiting for transfers between devices, per_device(): metric_all = lax.all_gather(metric_inv, AXES, axis=0, tiled=True)  49.4 us
    pallas_call x1, Pallas kernels, fit_rows(): pl.pallas_call(functools.partial(fit_kernel, (orbs, aux_n, dom_n, width,...  46.9 us
    all_to_all x1, blocking collectives, per_device(): small = lax.all_to_all(small, AXES, split_axis=0, concat_axis=0, tiled=True)  21.2 us
    pallas_call x1, Pallas kernels, gather_rows(): pl.pallas_call(functools.partial(gather_rows_kernel, batch, span, half_la...  14.3 us
    all_to_all x1, waiting for transfers between devices, per_device(): lax.all_to_all(turned, AXES, split_axis=0, concat_axis=0, tiled=True)  12.7 us
    all_to_all x1, starting transfers between devices, per_device(): lax.all_to_all(turned, AXES, split_axis=0, concat_axis=0, tiled=True)  9.65 us
    all_to_all x1, starting transfers between devices, per_device(): lax.all_to_all(jnp.broadcast_to(energy, (devices, 1)), AXES, split_axis=0...  7.48 us
  transfers between devices with their start and end apart: 4, of which 3 were waited for; matrix products, arithmetic and copies ran while one was open for 2% of the time, Pallas kernels for 5%

profile of v1, /device:TPU:1, one launch (start us, length us, event | category | flops | bytes accessed | tf_op | source)
XLA Modules:
  0.0 281.0 jit_solution(7308928838223249760)
XLA Ops:
  7.2 0.0 all-gather.2.cloned.1.call-start
  7.2 0.7 all-gather.2.cloned.1.call-update
  7.9 0.7 convert_element_type.24
  8.6 0.1 reshape.70
  8.7 0.8 copy.52
  9.5 0.1 reshape.65
  9.6 0.1 pad.13.clone
  9.7 0.1 copy.53
  9.8 21.2 %all_to_all.28 = bf16[128,1,88]{2,1,0:T(2,128)(2,1)S(1)} all-to-all(bf16[128,1,88]{2,1,0:T(2,128)(2,1)S(1)} %copy.53), channel_id=1, replica_groups=mesh['orb'=32,'row'=4] {'orb','row'}, dimensions={0} | all-to-all | bytes 45056 | tf_op jit(solution)/shard_map/all_to_all | solution.py:199
  31.0 0.1 copy.54
  31.1 0.1 copy.57
  31.2 0.7 reshape.68
  31.9 49.4 %all-gather.2.cloned.1.call-done.metric_ref = bf16[128,128,128]{2,1,0:T(8,128)(2,1)} async-done(((bf16[1,128,128]{2,1,0:T(8,128)(2,1)}), bf16[128,128,128]{2,1,0:T(8,128)(2,1)}) %all-gather.2.cloned.1.call-update) | async-done | bytes 4194320 | tf_op jit(solution)/shard_map/all_gather | solution.py:193
  81.3 46.9 %fit_rows.1 = (bf16[32,128,896]{2,1,0:T(8,128)(2,1)}, f32[1,1]{1,0:T(1,128)}) custom-call(s32[2,12]{1,0:T(2,128)} %dom_ref.1, s32[2,16]{1,0:T(2,128)} %aux_ref.1, s32[2]{0:T(128)} %count_ref.1, bf16[2,2048,1536]{2,1,0:T(8,128)(2,1)} %half_ref.1, bf16[128,128,128]{2,1,0:T(8,128)(2,1)} %all-gather.2.cloned.1.call-done.metric_ref, f32[2,32,1,128]{3,2,1,0:T(1,128)} %bitcast.33), custom_call_target="tpu_custom_call" | custom-call | tf_op jit(solution)/shard_map/fit_rows/pallas_call | solution.py:66
  128.2 5.8 %all-to-all-start.1 = ((bf16[128,32,896]{2,1,0:T(8,128)(2,1)}), bf16[128,32,896]{2,1,0:T(8,128)(2,1)}, u32[]{:S(2)}, u32[]{:S(2)}) async-start(bf16[128,32,896]{2,1,0:T(8,128)(2,1)} %bitcast.32), calls=%async_computation.1 | async-start | bytes 14680064 | tf_op jit(solution)/shard_map/all_to_all | solution.py:207
  134.5 0.1 copy.55
  134.6 87.8 %all-to-all-done.1.arrived_ref = bf16[128,32,896]{2,1,0:T(8,128)(2,1)} async-done(((bf16[128,32,896]{2,1,0:T(8,128)(2,1)}), bf16[128,32,896]{2,1,0:T(8,128)(2,1)}, u32[]{:S(2)}, u32[]{:S(2)}) %all-to-all-start.1) | async-done | bytes 7340064 | tf_op jit(solution)/shard_map/all_to_all | solution.py:207
  222.4 1.3 broadcast_in_dim.14
  223.7 7.5 %all-to-all-start.3 = ((f32[128,1,1]{2,1,0:T(1,128)}), f32[128,1,1]{2,1,0:T(1,128)S(1)}, u32[]{:S(2)}, u32[]{:S(2)}) async-start(f32[128,1,1]{2,1,0:T(1,128)} %broadcast_in_dim.14), calls=%async_computation.3 | async-start | bytes 131072 | tf_op jit(solution)/shard_map/all_to_all | solution.py:210
  231.1 0.6 broadcast_add_fusion.ids_ref
  231.8 14.3 %gather_rows.1 = (f32[32,4096]{1,0:T(8,128)}, f32[128,8,128]{2,1,0:T(8,128)}) custom-call(s32[128,7]{1,0:T(8,128)} %broadcast_add_fusion.ids_ref, bf16[128,32,896]{2,1,0:T(8,128)(2,1)} %all-to-all-done.1.arrived_ref), custom_call_target="tpu_custom_call" | custom-call | tf_op jit(solution)/shard_map/gather_rows/pallas_call | solution.py:136
  246.0 0.0 all-to-all-done.3
  246.0 9.7 %all-to-all-start.2 = ((f32[128,8,128]{2,1,0:T(8,128)}), f32[128,8,128]{2,1,0:T(8,128)S(1)}, u32[]{:S(2)}, u32[]{:S(2)}) async-start(f32[128,8,128]{2,1,0:T(8,128)} %get-tuple-element.8), calls=%async_computation.2 | async-start | bytes 1048576 | tf_op jit(solution)/shard_map/all_to_all | solution.py:220
  255.7 0.7 reduce_sum.79
  257.1 12.7 %all-to-all-done.2.tiles_ref = f32[128,8,128]{2,1,0:T(8,128)S(1)} async-done(((f32[128,8,128]{2,1,0:T(8,128)}), f32[128,8,128]{2,1,0:T(8,128)S(1)}, u32[]{:S(2)}, u32[]{:S(2)}) %all-to-all-start.2) | async-done | bytes 524320 | tf_op jit(solution)/shard_map/all_to_all | solution.py:220
  269.8 0.0 copy-start
  269.8 0.8 copy-done
  270.6 2.5 finish.1
  (30 shorter events, 0.2 us)
Async XLA Ops:
  7.2 74.2 %all-gather.2.cloned.1.call-start = ((), (), s32[]{:S(2)}) async-start(), calls=%async_computation.4 | async-start | bytes 4227072 | tf_op jit(solution)/shard_map/all_gather | solution.py:193
  128.2 94.1 %all-to-all-start.1 = ((bf16[128,32,896]{2,1,0:T(8,128)(2,1)}), bf16[128,32,896]{2,1,0:T(8,128)(2,1)}, u32[]{:S(2)}, u32[]{:S(2)}) async-start(bf16[128,32,896]{2,1,0:T(8,128)(2,1)} %bitcast.32), calls=%async_computation.1 | async-start | bytes 14680064 | tf_op jit(solution)/shard_map/all_to_all | solution.py:207
  223.7 22.4 %all-to-all-start.3 = ((f32[128,1,1]{2,1,0:T(1,128)}), f32[128,1,1]{2,1,0:T(1,128)S(1)}, u32[]{:S(2)}, u32[]{:S(2)}) async-start(f32[128,1,1]{2,1,0:T(1,128)} %broadcast_in_dim.14), calls=%async_computation.3 | async-start | bytes 131072 | tf_op jit(solution)/shard_map/all_to_all | solution.py:210
  246.0 23.8 %all-to-all-start.2 = ((f32[128,8,128]{2,1,0:T(8,128)}), f32[128,8,128]{2,1,0:T(8,128)S(1)}, u32[]{:S(2)}, u32[]{:S(2)}) async-start(f32[128,8,128]{2,1,0:T(8,128)} %get-tuple-element.8), calls=%async_computation.2 | async-start | bytes 1048576 | tf_op jit(solution)/shard_map/all_to_all | solution.py:220
  269.8 0.8 copy-start
Sparse Core Ops, SparseCore 0:
  11.1 70.1 all-gather.1

commit v2 on v1

v2 whole, which is shorter than its diff:
```python
import functools

import jax
import jax.numpy as jnp
from jax import lax
from jax.experimental import pallas as pl
from jax.experimental.pallas import tpu as pltpu
from jax.sharding import PartitionSpec as P

AXES = ("orb", "row")

MESH = pl.DeviceIdType.MESH


def spread_kernel(shape, parts, metric_ref, small_ref, all_ref, arrived_ref, part_send, part_recv, own_sem, small_sem):
    ny, nz, nc, nx = shape
    orb, x = lax.axis_index("orb"), lax.axis_index("row")
    c = lax.rem(orb, nc)
    z = lax.rem(orb // nc, nz)
    y = orb // (nc * nz)
    count = ny * nz * nc * nx
    me = orb * nx + x
    where = {"x": x, "y": y, "z": z}
    extent = {"x": nx, "y": ny, "z": nz}

    def device(y, z, c, x):
        return ((y * nz + z) * nc + c, x)

    def other(step):
        at = lax.rem(me + step, count)
        return at, (at // nx, lax.rem(at, nx))

    barrier = pltpu.get_barrier_semaphore()

    def greet(step, carry):
        pl.semaphore_signal(barrier, inc=1, device_id=other(step)[1], device_id_type=MESH)
        return carry

    lax.fori_loop(1, count, greet, 0)
    pl.semaphore_wait(barrier, count - 1)

    def region(gathered, rows):
        index = [pl.ds(0, extent[axis]) if axis in gathered else where[axis] for axis in ("y", "z")]
        last = pl.ds(0, nx) if "x" in gathered else x
        return all_ref.at[index[0], index[1], c, last, rows]

    orders = (("x", "y", "z"), ("y", "z", "x"), ("z", "x", "y"))
    own = pltpu.make_async_copy(metric_ref.at[0], all_ref.at[y, z, c, x], own_sem.at[0])
    own.start()
    started = []
    first = 0

    def ring(part, stage, rows):
        axis = orders[part][stage]
        copies = []
        for step in (2, 1, 3):
            at = dict(where)
            at[axis] = lax.rem(where[axis] + step, extent[axis])
            target = region(orders[part][:stage], rows)
            source = metric_ref.at[0, rows] if stage == 0 else target
            copies.append(
                pltpu.make_async_remote_copy(
                    src_ref=source,
                    dst_ref=target,
                    send_sem=part_send.at[part, stage, step - 1],
                    recv_sem=part_recv.at[part, stage, step - 1],
                    device_id=device(at["y"], at["z"], c, at["x"]),
                    device_id_type=MESH,
                )
            )
        return copies

    rows_of = []
    for part in range(3):
        rows_of.append(pl.ds(first, parts[part]))
        first += parts[part]
    flying = []
    for part in range(3):
        flying.append(ring(part, 0, rows_of[part]))
        for copy in flying[part]:
            copy.start()
        started += flying[part]

    def send_small(step, carry):
        at, target = other(step)
        pltpu.make_async_remote_copy(
            src_ref=small_ref.at[at],
            dst_ref=arrived_ref.at[me],
            send_sem=small_sem.at[0],
            recv_sem=small_sem.at[1],
            device_id=target,
            device_id_type=MESH,
        ).start()
        return carry

    lax.fori_loop(1, count, send_small, 0)
    own_small = pltpu.make_async_copy(small_ref.at[me], arrived_ref.at[me], own_sem.at[1])
    own_small.start()
    own.wait()

    for stage in range(1, 4):
        for part in range(3):
            for copy in flying[part]:
                copy.wait_recv()
            if stage < 3:
                flying[part] = ring(part, stage, rows_of[part])
            else:
                target = region(("x", "y", "z"), rows_of[part])
                flying[part] = [
                    pltpu.make_async_remote_copy(
                        src_ref=target,
                        dst_ref=target,
                        send_sem=part_send.at[part, 3, 0],
                        recv_sem=part_recv.at[part, 3, 0],
                        device_id=device(y, z, 1 - c, x),
                        device_id_type=MESH,
                    )
                ]
            for copy in flying[part]:
                copy.start()
            started += flying[part]
    for part in range(3):
        for copy in flying[part]:
            copy.wait_recv()
    for copy in started:
        copy.wait_send()
    own_small.wait()
    pltpu.make_async_remote_copy(
        src_ref=small_ref.at[pl.ds(0, count - 1)],
        dst_ref=arrived_ref.at[pl.ds(0, count - 1)],
        send_sem=small_sem.at[0],
        recv_sem=small_sem.at[1],
        device_id=other(1)[1],
        device_id_type=MESH,
    ).wait()


def spread(metric_inv, small, shape):
    width = metric_inv.shape[1]
    third = (width // 3 + 15) // 16 * 16
    return pl.pallas_call(
        functools.partial(spread_kernel, shape, (third, third, width - 2 * third)),
        in_specs=[pl.BlockSpec(memory_space=pltpu.VMEM)] * 2,
        out_specs=[pl.BlockSpec(memory_space=pltpu.VMEM)] * 2,
        out_shape=[
            jax.ShapeDtypeStruct(shape + metric_inv.shape[1:], metric_inv.dtype),
            jax.ShapeDtypeStruct(small.shape, small.dtype),
        ],
        scratch_shapes=[
            pltpu.SemaphoreType.DMA((3, 4, 3)),
            pltpu.SemaphoreType.DMA((3, 4, 3)),
            pltpu.SemaphoreType.DMA((2,)),
            pltpu.SemaphoreType.DMA((2,)),
        ],
        compiler_params=pltpu.CompilerParams(collective_id=0, has_side_effects=True),
        name="spread",
    )(metric_inv, small)


def exchange_kernel(
    shape, dom_ref, aux_ref, row_ref, live_ref, half_ref, metric_ref, small_ref, arrived_ref, energy_ref,
    fitted, coef_dom, stage, send_sem, recv_sem, own_sem,
):
    orbs, aux_n, dom_n, width, span, group, blocks, quarters, torus = shape
    step = pl.program_id(0)
    columns = dom_n * width
    rows = width // quarters
    count = blocks * quarters
    fit_steps = orbs * aux_n // group
    window = dom_n + span - 1
    ny, nz, nc = torus
    orb_at, x = lax.axis_index("orb"), lax.axis_index("row")
    me = orb_at * quarters + x
    c = lax.rem(orb_at, nc)
    z = lax.rem(orb_at // nc, nz)
    y = orb_at // (nc * nz)
    barrier = pltpu.get_barrier_semaphore()

    @pl.when(step == 0)
    def _():
        def greet(i, carry):
            at = lax.rem(me + i, count)
            pl.semaphore_signal(
                barrier, inc=1, device_id=(at // quarters, lax.rem(at, quarters)), device_id_type=MESH
            )
            return carry

        lax.fori_loop(1, count, greet, 0)
        energy_ref[...] = jnp.zeros_like(energy_ref)
        for orb in range(orbs):
            for k in range(dom_n):
                pieces = [
                    small_ref[dom_ref[orb, k] * quarters + q][:, orb * rows : (orb + 1) * rows]
                    for q in range(quarters)
                ]
                coef_dom[orb, :, k * width : (k + 1) * width] = jnp.concatenate(pieces, axis=1)

    @pl.when(step < fit_steps)
    def _():
        orb = step * group // aux_n
        first = step * group % aux_n
        energy = jnp.zeros((1, 1), jnp.float32)
        for g in range(group):
            a = first + g
            factor = metric_ref[aux_ref[orb, a]]
            block = jnp.dot(
                factor, half_ref[0, g * width : (g + 1) * width], preferred_element_type=jnp.float32
            )
            block = (block * live_ref[orb * aux_n + a][:, 0:1]).astype(jnp.bfloat16)
            at = pl.ds(pl.multiple_of(a * width, width), width)
            for j in range(window):
                k = j % dom_n
                fitted[orb * window + j, at] = block[:, k * width : (k + 1) * width]
            weighted = block.astype(jnp.float32) * coef_dom[orb]
            projected = jnp.sum(weighted, axis=1, keepdims=True)
            energy += jnp.sum(projected * projected, axis=0, keepdims=True)
        energy_ref[...] += jnp.broadcast_to(energy, energy_ref.shape)

    @pl.when(step == fit_steps)
    def _():
        pl.semaphore_wait(barrier, count - 1)

    def target(i):
        ty = lax.rem(y + i, ny)
        tz = lax.rem(z + i + i // ny, nz)
        tc = lax.rem(c + i // (ny * nz), nc)
        return (ty * nz + tz) * nc + tc

    @pl.when(step > fit_steps)
    def _():
        i = step - fit_steps - 1
        block = target(i)
        for q in range(quarters):
            part = stage.at[i, q * rows : (q + 1) * rows]
            here = jnp.logical_and(block == orb_at, x == q)

            @pl.when(here)
            def _():
                pltpu.make_async_copy(part, arrived_ref.at[me], own_sem).start()

            @pl.when(jnp.logical_not(here))
            def _():
                pltpu.make_async_remote_copy(
                    src_ref=part,
                    dst_ref=arrived_ref.at[me],
                    send_sem=send_sem,
                    recv_sem=recv_sem,
                    device_id=(block, q),
                    device_id_type=MESH,
                ).start()

    @pl.when(jnp.logical_and(step >= fit_steps, step < fit_steps + blocks))
    def _():
        i = step - fit_steps
        block = target(i)
        first = row_ref[block]
        left = fitted[first]
        right = jnp.concatenate([fitted[first + j] for j in range(span)], axis=1)
        out = lax.dot_general(left, right, (((0,), (0,)), ((), ())), preferred_element_type=jnp.float32)
        stage[i] = out.astype(jnp.bfloat16)

    @pl.when(step == fit_steps + blocks)
    def _():
        pltpu.make_async_copy(stage.at[0, 0:rows], arrived_ref.at[me], own_sem).wait()
        others = arrived_ref.at[pl.ds(0, count - 1)]
        pltpu.make_async_remote_copy(
            src_ref=others,
            dst_ref=others,
            send_sem=send_sem,
            recv_sem=recv_sem,
            device_id=(lax.rem(orb_at + 1, blocks), x),
            device_id_type=MESH,
        ).wait()


def exchange(half_ints, metric_all, small, basis_domain, aux_domain, aux_count, basis_blocks, torus):
    orbs, aux_rows, columns = half_ints.shape
    devices, width = metric_all.shape[:2]
    aux_n, dom_n = aux_domain.shape[1], basis_domain.shape[1]
    span = dom_n // 2 + 1
    group = 4
    quarters = devices // basis_blocks
    rows = width // quarters
    fit_steps = orbs * aux_n // group
    per_orb = aux_n // group

    def half_map(step):
        at = jnp.minimum(step, fit_steps - 1)
        return (at // per_orb, at % per_orb, 0)

    window = dom_n + span - 1
    start = jnp.arange(orbs * dom_n, dtype=jnp.int32)
    start = start // dom_n * window + start % dom_n
    block_ids = jnp.arange(basis_blocks, dtype=jnp.int32)
    found = basis_domain.reshape(1, orbs * dom_n) == block_ids[:, None]
    row_at = jnp.sum(jnp.where(found, start[None], 0), axis=1)
    live = jnp.arange(aux_n, dtype=jnp.int32)[None, :] < aux_count[:, None]
    live = jnp.broadcast_to(live.astype(jnp.float32).reshape(orbs * aux_n, 1, 1), (orbs * aux_n, 1, width))
    vmem = pl.BlockSpec(memory_space=pltpu.VMEM)
    smem = pl.BlockSpec(memory_space=pltpu.SMEM)
    return pl.pallas_call(
        functools.partial(
            exchange_kernel, (orbs, aux_n, dom_n, width, span, group, basis_blocks, quarters, torus)
        ),
        grid=(fit_steps + basis_blocks + 1,),
        in_specs=[smem, smem, smem, vmem, pl.BlockSpec((1, group * width, columns), half_map), vmem, vmem],
        out_specs=[pl.BlockSpec(memory_space=pl.ANY), pl.BlockSpec((1, width), lambda step: (0, 0))],
        out_shape=[
            jax.ShapeDtypeStruct((devices, rows, span * width), jnp.bfloat16),
            jax.ShapeDtypeStruct((1, width), jnp.float32),
        ],
        scratch_shapes=[
            pltpu.VMEM((orbs * window, aux_rows, width), jnp.bfloat16),
            pltpu.VMEM((orbs, 1, columns), jnp.float32),
            pltpu.VMEM((basis_blocks, width, span * width), jnp.bfloat16),
            pltpu.SemaphoreType.DMA,
            pltpu.SemaphoreType.DMA,
            pltpu.SemaphoreType.DMA,
        ],
        compiler_params=pltpu.CompilerParams(
            collective_id=1,
            has_side_effects=True,
            vmem_limit_bytes=60 * 1024 * 1024,
            dimension_semantics=("arbitrary",),
        ),
        name="exchange",
    )(basis_domain, aux_domain, row_at, live, half_ints, metric_all, small)


def gather_rows_kernel(batch, span, half_last, ids_ref, arrived_ref, total_ref, turned_ref, acc):
    step = pl.program_id(0)
    blocks = acc.shape[0] - 1
    rows, width = acc.shape[1], acc.shape[2]
    quarters = width // rows

    @pl.when(step == 0)
    def _():
        acc[...] = jnp.zeros_like(acc)

    for s in range(batch):
        places = [ids_ref[step * batch + s, j] for j in range(span)]
        sums = []
        for j in range(span):
            part = arrived_ref[s, :, j * width : (j + 1) * width].astype(jnp.float32)
            if j == 0 or (half_last and j == span - 1):
                part = part * 0.5
            sums.append(acc[places[j]] + part)
        for j in range(span):
            acc[places[j]] = sums[j]

    @pl.when(step == pl.num_programs(0) - 1)
    def _():
        for block in range(blocks):
            total_ref[:, block * width : (block + 1) * width] = acc[block]
        for group in range(blocks // quarters):
            tall = acc[group * quarters : (group + 1) * quarters].reshape(quarters * rows, width)
            turned = tall.T
            for beta in range(quarters):
                piece = turned[:, beta * rows : (beta + 1) * rows]
                for q in range(quarters):
                    tile = piece[q * rows : (q + 1) * rows]
                    packed = jnp.concatenate(
                        [tile[a * 8 : (a + 1) * 8] for a in range(rows // 8)], axis=1
                    )
                    turned_ref[(group * quarters + beta) * quarters + q] = packed


def gather_rows(ids, arrived, basis_blocks, half_last):
    devices, rows, columns = arrived.shape
    span = ids.shape[1]
    width = columns // span
    batch = 8
    return pl.pallas_call(
        functools.partial(gather_rows_kernel, batch, span, half_last),
        grid_spec=pltpu.PrefetchScalarGridSpec(
            num_scalar_prefetch=1,
            grid=(devices // batch,),
            in_specs=[pl.BlockSpec((batch, rows, columns), lambda step, ids: (step, 0, 0))],
            out_specs=[
                pl.BlockSpec((rows, basis_blocks * width), lambda step, ids: (0, 0)),
                pl.BlockSpec((devices, 8, width), lambda step, ids: (0, 0, 0)),
            ],
            scratch_shapes=[pltpu.VMEM((basis_blocks + 1, rows, width), jnp.float32)],
        ),
        out_shape=[
            jax.ShapeDtypeStruct((rows, basis_blocks * width), jnp.float32),
            jax.ShapeDtypeStruct((devices, 8, width), jnp.float32),
        ],
        compiler_params=pltpu.CompilerParams(dimension_semantics=("arbitrary",)),
        name="gather_rows",
    )(ids, arrived)


def finish_kernel(quarters, total_ref, turned_ref, energy_ref, out_ref, mean_ref, tiles, energies, sems, own_sems):
    rows, columns = total_ref.shape
    width = turned_ref.shape[2]
    count = turned_ref.shape[0]
    me = lax.axis_index("orb") * quarters + lax.axis_index("row")

    def other(step):
        at = lax.rem(me + step, count)
        return at, (at // quarters, lax.rem(at, quarters))

    barrier = pltpu.get_barrier_semaphore()

    def greet(step, carry):
        pl.semaphore_signal(barrier, inc=1, device_id=other(step)[1], device_id_type=MESH)
        return carry

    lax.fori_loop(1, count, greet, 0)
    pl.semaphore_wait(barrier, count - 1)
    own = [
        pltpu.make_async_copy(turned_ref.at[me], tiles.at[me], own_sems.at[0]),
        pltpu.make_async_copy(energy_ref, energies.at[me], own_sems.at[1]),
    ]
    for copy in own:
        copy.start()

    def send(step, carry):
        at, device = other(step)
        pltpu.make_async_remote_copy(
            src_ref=turned_ref.at[at],
            dst_ref=tiles.at[me],
            send_sem=sems.at[0],
            recv_sem=sems.at[1],
            device_id=device,
            device_id_type=MESH,
        ).start()
        pltpu.make_async_remote_copy(
            src_ref=energy_ref,
            dst_ref=energies.at[me],
            send_sem=sems.at[2],
            recv_sem=sems.at[3],
            device_id=device,
            device_id_type=MESH,
        ).start()
        return carry

    lax.fori_loop(1, count, send, 0)
    for copy in own:
        copy.wait()
    for k, ref in enumerate((tiles, energies)):
        part = ref.at[pl.ds(0, count - 1)]
        pltpu.make_async_remote_copy(
            src_ref=part,
            dst_ref=part,
            send_sem=sems.at[2 * k],
            recv_sem=sems.at[2 * k + 1],
            device_id=other(1)[1],
            device_id_type=MESH,
        ).wait()
    for block in range(columns // width):
        for a in range(rows // 8):
            strip = jnp.concatenate(
                [tiles[block * quarters + q, :, a * rows : (a + 1) * rows] for q in range(quarters)],
                axis=1,
            )
            at = slice(a * 8, (a + 1) * 8), slice(block * width, (block + 1) * width)
            out_ref[at] = total_ref[at] + strip
    mean_ref[...] = jnp.sum(energies[...], axis=0)


def finish(total, turned, energy, quarters):
    devices, _, width = turned.shape
    return pl.pallas_call(
        functools.partial(finish_kernel, quarters),
        in_specs=[pl.BlockSpec(memory_space=pltpu.VMEM)] * 3,
        out_specs=[pl.BlockSpec(memory_space=pltpu.VMEM)] * 2,
        out_shape=[
            jax.ShapeDtypeStruct(total.shape, jnp.float32),
            jax.ShapeDtypeStruct((1, width), jnp.float32),
        ],
        scratch_shapes=[
            pltpu.VMEM(turned.shape, jnp.float32),
            pltpu.VMEM((devices, 1, width), jnp.float32),
            pltpu.SemaphoreType.DMA((4,)),
            pltpu.SemaphoreType.DMA((2,)),
        ],
        compiler_params=pltpu.CompilerParams(collective_id=2, has_side_effects=True),
        name="finish",
    )(total, turned, energy)


def per_device(half_ints, metric_inv, coefficients, basis_domain, aux_domain, aux_count):
    devices = lax.axis_size(AXES)
    me = lax.axis_index(AXES)
    orbs = half_ints.shape[0]
    width = metric_inv.shape[1]
    rows = coefficients.shape[0]
    basis_blocks = rows * devices // width
    quarters = width // rows
    dom_n = basis_domain.shape[1]
    span = dom_n // 2 + 1

    coef_send = coefficients.T.reshape(devices, orbs * rows).astype(jnp.float32)
    dom_send = jnp.broadcast_to(
        basis_domain.reshape(1, orbs * dom_n).astype(jnp.float32), (devices, orbs * dom_n)
    )
    small = jnp.concatenate([coef_send, dom_send], axis=1)
    small = jnp.pad(small, ((0, 0), (0, width - small.shape[1]))).reshape(devices, 1, width)
    torus = (4, 4, 2)
    metric_all, small = spread(metric_inv, small, torus + (quarters,))
    metric_all = metric_all.reshape(devices, width, width)
    arrived, energy = exchange(
        half_ints, metric_all, small, basis_domain, aux_domain, aux_count, basis_blocks, torus
    )
    domains = small[:, 0, orbs * rows : orbs * (rows + dom_n)].astype(jnp.int32)
    place = jnp.arange(orbs * dom_n, dtype=jnp.int32)[None, :]
    hits = domains == me // quarters
    at = jnp.sum(jnp.where(hits, place + 1, 0), axis=1) - 1
    turn = jnp.arange(span, dtype=jnp.int32)[None, :]
    wanted = jnp.where(at[:, None] < 0, -1, at[:, None] // dom_n * dom_n + (at[:, None] + turn) % dom_n)
    picked = wanted[:, :, None] == place[None]
    ids = jnp.sum(jnp.where(picked, domains[:, None, :] - basis_blocks, 0), axis=2) + basis_blocks
    total, turned = gather_rows(ids, arrived, basis_blocks, dom_n % 2 == 0)
    out, mean = finish(total, turned, energy, quarters)
    return out, mean[0, 0] / (orbs * devices)


def solution(mesh):
    in_specs = (
        P(AXES, None, None),
        P(AXES, None, None),
        P(AXES, None),
        P(AXES, None),
        P(AXES, None),
        P(AXES),
    )
    out_specs = (P(AXES, None), P())
    return jax.shard_map(
        per_device, mesh=mesh, in_specs=in_specs, out_specs=out_specs, check_vma=False
    )
```

time: 282 us -> 199 us (0.71)
  waiting for transfers between devices: 151 us -> 0 us
  Pallas kernels: 63.6 us -> 186 us
  starting transfers between devices: 23 us -> 0 us
  blocking collectives: 21.2 us -> 0 us
  between operations: 16.1 us -> 2.48 us
    pallas_call x2 -> x3, Pallas kernels: 49.4 us -> 173 us  [the longest x1 115 us: exchange(): pl.pallas_call(functools.partial(exchange_kernel, (orbs, aux_n, dom_n, wi...]
    all_to_all x3 -> x0, waiting for transfers between devices: 100 us -> none  [the longest x1 87.8 us: per_device(): lax.all_to_all(send.reshape(devices, rows, span * width), AXES, split_axi...]
    all_gather x1 -> x0, waiting for transfers between devices: 49.4 us -> none  [per_device(): metric_all = lax.all_gather(metric_inv, AXES, axis=0, tiled=True)]
    all_to_all x3 -> x0, starting transfers between devices: 23 us -> none  [the longest x1 9.65 us: per_device(): lax.all_to_all(turned, AXES, split_axis=0, concat_axis=0, tiled=True)]
    all_to_all x1 -> x0, blocking collectives: 21.2 us -> none  [per_device(): small = lax.all_to_all(small, AXES, split_axis=0, concat_axis=0, tiled=True)]
  transfers between devices with their start and end apart: 4 -> 0, of which waited for: 3 -> 0; matrix products, arithmetic and copies ran while one was open for 2% -> 0% of each run, Pallas kernels for 5% -> 0%
where the time goes in v2:
time: 199 us; the launch traced here: 198 us
  Pallas kernels  186 us (93%)
  other arithmetic  4.96 us (2%)
  local copies, waits for them, and re-layouts  4.57 us (2%)
  between operations  2.48 us (1%)
    pallas_call x1, Pallas kernels, exchange(): pl.pallas_call(functools.partial(exchange_kernel, (orbs, aux_n, dom_n, wi...  115 us
    pallas_call x1, Pallas kernels, spread(): pl.pallas_call(functools.partial(spread_kernel, shape, (third, third, wid...  35.4 us
    pallas_call x1, Pallas kernels, finish(): pl.pallas_call(functools.partial(finish_kernel, quarters), in_specs=[pl.B...  22.5 us
    pallas_call x1, Pallas kernels, gather_rows(): pl.pallas_call(functools.partial(gather_rows_kernel, batch, span, half_la...  13 us

profile of v2, /device:TPU:1, one launch (start us, length us, event | category | flops | bytes accessed | tf_op | source)
XLA Modules:
  0.0 198.0 jit_solution(8373394799346696774)
XLA Ops:
  0.6 0.8 reshape.159
  1.4 0.1 pad.6.clone
  1.5 0.6 select_reduce_fusion.1.row_ref
  2.1 0.7 compare_convert_fusion
  2.8 0.1 reshape.163
  2.9 0.7 broadcast_in_dim.81.live_ref
  3.6 0.7 convert_bitcast_fusion
  4.3 0.1 copy.15
  4.4 0.1 reshape.162
  4.5 0.6 pad.4
  5.2 35.4 %spread.1 = (bf16[4,4,2,4,128,128]{5,4,3,2,1,0:T(8,128)(2,1)}, f32[128,1,128]{2,1,0:T(1,128)}) custom-call(bf16[1,128,128]{2,1,0:T(8,128)(2,1)} %metric_ref.1, f32[128,1,128]{2,1,0:T(1,128)} %bitcast.10), custom_call_target="tpu_custom_call" | custom-call | tf_op jit(solution)/shard_map/spread/pallas_call | solution.py:141
  40.6 1.0 convert_compare_fusion
  41.7 0.1 copy.16
  41.8 0.1 select_reduce_fusion.2
  41.9 1.0 convert_add_fusion
  43.0 0.1 copy.17
  43.1 0.1 copy.18
  43.2 0.6 broadcast_add_fusion.ids_ref
  43.8 115.0 %exchange.1 = (bf16[128,32,896]{2,1,0:T(8,128)(2,1)}, f32[1,128]{1,0:T(1,128)}) custom-call(s32[2,12]{1,0:T(2,128)} %dom_ref.1, s32[2,16]{1,0:T(2,128)} %aux_ref.1, s32[32]{0:T(128)} %select_reduce_fusion.1.row_ref, f32[32,1,128]{2,1,0:T(1,128)} %broadcast_in_dim.81.live_ref, bf16[2,2048,1536]{2,1,0:T(8,128)(2,1)} %half_ref.1, ...), custom_call_target="tpu_custom_call" | custom-call | tf_op jit(solution)/shard_map/exchange/pallas_call | solution.py:301
  158.8 13.0 %gather_rows.1 = (f32[32,4096]{1,0:T(8,128)}, f32[128,8,128]{2,1,0:T(8,128)}) custom-call(s32[128,7]{1,0:T(8,128)} %broadcast_add_fusion.ids_ref, bf16[128,32,896]{2,1,0:T(8,128)(2,1)} %get-tuple-element.12.arrived_ref), custom_call_target="tpu_custom_call" | custom-call | tf_op jit(solution)/shard_map/gather_rows/pallas_call | solution.py:373
  171.8 22.5 %finish.1 = (f32[32,4096]{1,0:T(8,128)}, f32[1,128]{1,0:T(1,128)}) custom-call(f32[32,4096]{1,0:T(8,128)} %get-tuple-element.13.total_ref, f32[128,8,128]{2,1,0:T(8,128)} %get-tuple-element.14.turned_ref, f32[1,128]{1,0:T(1,128)} %get-tuple-element.15.energy_ref), custom_call_target="tpu_custom_call" | custom-call | tf_op jit(solution)/shard_map/finish/pallas_call | solution.py:465
  195.0 1.9 copy.21
  (8 shorter events, 0.1 us)
